TPU v7x, 32 devices: a whole 2x2x4 slice. The times are simulated.
32 devices in a mesh: gx: 2 (over core), gy: 4 (over y, x), ma: 4 (over z).
Axes of the slice: x: 2, y: 2, z: 4, core: 2. Of those that a mesh axis runs over, the one named last changes fastest.
Arguments:
- object_field: float32 [2, 256, 1024], P(None, 'gx', 'gy'), may hold values from -5 to 5
- probe_modes: float32 [8, 2, 256, 256], P('ma'), may hold values from -1.5 to 1.5
- measured: float32 [2, 4, 2, 256, 256], P('gx', 'gy'), may hold values from 0.1 to 4
- positions: int32 [2, 4, 2, 2], P('gx', 'gy'), may hold values from 0 to 255, as said below
- slot_counts: int32 [2, 4], P('gx', 'gy'), may hold values from 1 to 2, as said below
Outputs:
- updated_object: float32 [2, 256, 1024], P(None, 'gx', 'gy')
Inputs may be any that keep to these rules, and one draw needn't show every extreme that they name: positions[a, b, s] holds a row 0 to 127 and a column 0 to 255 of tile (a, b); slots s >= slot_counts[a, b] are unused. `slot_counts`: some tile uses all 2 slots.
All inputs are finite; a program needn't handle non-finite values.
Results may differ from a plain program's by a relative error of at most 0.0023.
Values sent between devices are 32-bit elements; how exact they have to be, the bound alone decides.
A program may use at most 64 MiB of HBM per device.

v0:
```python
import math
import jax
import jax.numpy as jnp
from jax import lax
from jax.sharding import PartitionSpec as P

OUTER = 2
DAMPING = 1.0


def padded_2(block, sides, width):
    for axis, dim in sides:
        count = lax.axis_size(axis)
        forward = [(i, i + 1) for i in range(count - 1)]
        backward = [(target, source) for source, target in forward]
        low = lax.ppermute(
            lax.slice_in_dim(block, block.shape[dim] - width, None, axis=dim), axis, forward
        )
        high = lax.ppermute(lax.slice_in_dim(block, 0, width, axis=dim), axis, backward)
        block = jnp.concatenate([low, block, high], axis=dim)
    return block


def dft_tables(patch_width):
    ladder = jnp.arange(patch_width, dtype=jnp.int32)
    phases = ladder[:, None] * ladder[None, :] % patch_width
    angles = phases.astype(jnp.float32) * (2.0 * math.pi / patch_width)
    factor = 1.0 / math.sqrt(patch_width)
    real_part = jnp.cos(angles) * factor
    imag_part = -jnp.sin(angles) * factor
    table_one = jnp.concatenate(
        [jnp.concatenate([real_part, -imag_part], 1), jnp.concatenate([imag_part, real_part], 1)], 0
    ).astype(jnp.bfloat16)
    table_two = jnp.concatenate(
        [jnp.concatenate([real_part, imag_part], 1), jnp.concatenate([-imag_part, real_part], 1)], 0
    ).astype(jnp.bfloat16)
    return (table_one, table_two)


def forward_transform(wavefield, tables):
    patch_width = wavefield.shape[-1]
    halfway = jnp.einsum(
        "pqci,bcik->bpqk",
        tables[0].reshape(2, patch_width, 2, patch_width),
        wavefield,
        preferred_element_type=jnp.float32,
    ).astype(jnp.bfloat16)
    return jnp.einsum(
        "bcik,ckl->bil",
        halfway,
        tables[1].reshape(2, patch_width, 2 * patch_width),
        preferred_element_type=jnp.float32,
    )


def adjoint_transform(weighted, tables):
    patch_width = weighted.shape[1]
    halfway = jnp.einsum(
        "bik,kl->bil", weighted, tables[0], preferred_element_type=jnp.float32
    ).astype(jnp.bfloat16)
    return jnp.einsum(
        "pqci,bicl->bpql",
        tables[1].reshape(2, patch_width, 2, patch_width),
        halfway.reshape(halfway.shape[0], patch_width, 2, patch_width),
        preferred_element_type=jnp.float32,
    )


def exit_waves(probe_modes, windows):
    probe_real = probe_modes[None, :, 0]
    probe_imag = probe_modes[None, :, 1]
    window_real = windows[:, None, 0]
    window_imag = windows[:, None, 1]
    real_part = probe_real * window_real - probe_imag * window_imag
    imag_part = probe_real * window_imag + probe_imag * window_real
    wavefield = jnp.stack([real_part, imag_part], 2).astype(jnp.bfloat16)
    return wavefield.reshape(-1, 2, probe_modes.shape[-1], probe_modes.shape[-1])


def intensity_part(spectra, mode_count):
    patch_width = spectra.shape[1]
    grouped = spectra.reshape(-1, mode_count, patch_width, 2 * patch_width)
    squared = grouped * grouped
    return jnp.sum(squared[..., :patch_width] + squared[..., patch_width:], axis=1)


def change_part(spectra, moved_spectra, mode_count):
    patch_width = spectra.shape[1]
    grouped = spectra.reshape(-1, mode_count, patch_width, 2 * patch_width)
    shifted = moved_spectra.reshape(-1, mode_count, patch_width, 2 * patch_width)
    product = grouped * shifted
    return 2.0 * jnp.sum(product[..., :patch_width] + product[..., patch_width:], axis=1)


def mode_images(weights, spectra, probe_modes, tables):
    mode_count = probe_modes.shape[0]
    patch_width = probe_modes.shape[-1]
    doubled = jnp.concatenate([weights, weights], -1)
    grouped = spectra.reshape(-1, mode_count, patch_width, 2 * patch_width)
    weighted = (2.0 * grouped * doubled[:, None]).astype(jnp.bfloat16)
    returned = adjoint_transform(weighted.reshape(-1, patch_width, 2 * patch_width), tables)
    returned = returned.reshape(-1, mode_count, 2, patch_width, patch_width)
    probe_real = probe_modes[None, :, 0]
    probe_imag = probe_modes[None, :, 1]
    real_part = jnp.sum(probe_real * returned[:, :, 0] + probe_imag * returned[:, :, 1], axis=1)
    imag_part = jnp.sum(probe_real * returned[:, :, 1] - probe_imag * returned[:, :, 0], axis=1)
    return jnp.stack([real_part, imag_part], 1)


def fold_edges(widened, axis_dim, length, rim_width):
    middle = lax.slice_in_dim(widened, 2 * rim_width, 2 * rim_width + length, axis=axis_dim)
    low_rim = lax.slice_in_dim(widened, 0, rim_width, axis=axis_dim)
    high_rim = lax.slice_in_dim(
        widened, length + 3 * rim_width, length + 4 * rim_width, axis=axis_dim
    )
    low_pads = [(0, 0), (0, 0), (0, 0)]
    high_pads = [(0, 0), (0, 0), (0, 0)]
    low_pads[axis_dim] = (0, length - rim_width)
    high_pads[axis_dim] = (length - rim_width, 0)
    return middle + jnp.pad(low_rim, low_pads) + jnp.pad(high_rim, high_pads)


def shards(object_field, probe_modes, measured, positions, slot_counts):
    patch_width = probe_modes.shape[-1]
    mode_count = probe_modes.shape[0]
    rim_width = patch_width // 2
    tile_rows = object_field.shape[1]
    tile_cols = object_field.shape[2]
    slot_count = measured.shape[2]
    share_rows = tile_rows // lax.axis_size("ma")
    tables = dft_tables(patch_width)
    targets = measured[0, 0]
    centres = positions[0, 0]
    live_mask = (jnp.arange(slot_count, dtype=jnp.int32) < slot_counts[0, 0]).astype(jnp.float32)[
        :, None, None
    ]
    anchor = jnp.zeros((), jnp.int32)

    def spectra_of(current):
        padded = padded_2(current, (("gx", 1), ("gy", 2)), rim_width)
        windows = jnp.stack(
            [
                lax.dynamic_slice(
                    padded,
                    (anchor, centres[slot_index, 0], centres[slot_index, 1]),
                    (2, patch_width, patch_width),
                )
                for slot_index in range(slot_count)
            ],
            0,
        )
        return forward_transform(exit_waves(probe_modes, windows), tables)

    def mode_total(partial_value):
        return lax.psum(partial_value, "ma")

    def combine(folded):
        summed = lax.psum(folded, "ma")
        return summed

    def project(weights, spectra):
        pieces = mode_images(weights, spectra, probe_modes, tables)
        extended = jnp.zeros((2, tile_rows + patch_width, tile_cols + patch_width), jnp.float32)
        for slot_index in range(slot_count):
            corner = (anchor, centres[slot_index, 0], centres[slot_index, 1])
            extended = lax.dynamic_update_slice(
                extended,
                lax.dynamic_slice(extended, corner, (2, patch_width, patch_width))
                + pieces[slot_index],
                corner,
            )
        widened = padded_2(extended, (("gx", 1), ("gy", 2)), rim_width)
        folded = fold_edges(fold_edges(widened, 1, tile_rows, rim_width), 2, tile_cols, rim_width)
        result = combine(folded)
        return result

    def local_sum(first_vec, second_vec):
        first_vec = lax.dynamic_slice_in_dim(
            first_vec, lax.axis_index("ma") * share_rows, share_rows, 1
        )
        second_vec = lax.dynamic_slice_in_dim(
            second_vec, lax.axis_index("ma") * share_rows, share_rows, 1
        )
        return jnp.sum(first_vec * second_vec)

    current = object_field
    for outer_step in range(OUTER):
        spectra = spectra_of(current)
        misfit = live_mask * (mode_total(intensity_part(spectra, mode_count)) - targets)
        gradient = project(misfit, spectra)
        residual = -gradient
        direction = residual
        norm_now = lax.psum(local_sum(residual, residual), ("gx", "gy", "ma"))
        moved_spectra = spectra_of(direction)
        change = live_mask * mode_total(change_part(spectra, moved_spectra, mode_count))
        applied = project(change, spectra) + DAMPING * direction
        step_size = norm_now / lax.psum(local_sum(direction, applied), ("gx", "gy", "ma"))
        update = step_size * direction
        residual = residual - step_size * applied
        current = current + update
    return current


def solution(mesh):
    return jax.shard_map(
        shards,
        mesh=mesh,
        in_specs=(
            P(None, "gx", "gy"),
            P("ma", None, None, None),
            P("gx", "gy", None, None, None),
            P("gx", "gy", None, None),
            P("gx", "gy"),
        ),
        out_specs=P(None, "gx", "gy"),
        check_vma=False,
    )
```

profile of v0, /device:TPU:0, one launch (start us, length us, event | category | flops | bytes accessed | tf_op | source)
XLA Modules:
  0.0 797.4 jit_solution(15070351154825093424)
XLA Ops:
  45.2 36.4 %all-reduce.15.cloned.1.call-done = f32[2,256,256]{2,1,0:T(8,128)} async-done(((f32[2,256,256]{2,1,0:T(8,128)}), f32[2,256,256]{2,1,0:T(8,128)}) %all-reduce.15.cloned.1.call-update) | async-done | bytes 524304 | tf_op jit(solution)/shard_map/psum | solution.py:155
  89.5 7.8 dynamic_update_slice.24
  99.3 8.2 %dynamic_update_slice.25 = f32[2,384,512]{1,2,0:T(8,128)S(1)} dynamic-update-slice(f32[2,384,512]{1,2,0:T(8,128)S(1)} %dynamic_update_slice.24, f32[2,256,256]{1,2,0:T(8,128)} %fusion.50, s32[]{:T(128)} %constant.15.clone.1, s32[]{:T(128)S(6)} %select_n.33, s32[]{:T(128)S(6)} %select_n.34) | dynamic-update-slice | bytes 1048580 | tf_op jit(solution)/shard_map/dynamic_update_slice | solution.py:166
  117.4 12.9 %collective-permute-done.6 = f32[2,640,128]{1,2,0:T(8,128)S(1)} collective-permute-done((f32[2,640,128]{1,2,0:T(8,128)S(1)}, f32[2,640,128]{1,2,0:T(8,128)S(1)}, u32[]{:S(2)}, u32[]{:S(2)}) %collective-permute-start.6) | collective-permute-done | bytes 655392 | tf_op jit(solution)/shard_map/ppermute | solution.py:16
  130.4 16.7 %collective-permute-done.7 = f32[2,640,128]{1,2,0:T(8,128)S(1)} collective-permute-done((f32[2,640,128]{1,2,0:T(8,128)S(1)}, f32[2,640,128]{1,2,0:T(8,128)S(1)}, u32[]{:S(2)}, u32[]{:S(2)}) %collective-permute-start.7) | collective-permute-done | bytes 655392 | tf_op jit(solution)/shard_map/ppermute | solution.py:19
  148.6 33.7 %all-reduce.17.cloned.1.call-done = f32[2,128,256]{1,2,0:T(8,128)} async-done(((f32[2,128,256]{1,2,0:T(8,128)}), f32[2,128,256]{1,2,0:T(8,128)}) %all-reduce.17.cloned.1.call-update) | async-done | bytes 262160 | tf_op jit(solution)/shard_map/psum | solution.py:158
  193.0 7.2 collective-permute-done.10
  200.2 10.3 %collective-permute-done.11 = f32[2,384,128]{1,2,0:T(8,128)S(1)} collective-permute-done((f32[2,384,128]{1,2,0:T(8,128)S(1)}, f32[2,384,128]{1,2,0:T(8,128)S(1)}, u32[]{:S(2)}, u32[]{:S(2)}) %collective-permute-start.11) | collective-permute-done | bytes 393248 | tf_op jit(solution)/shard_map/ppermute | solution.py:19
  218.3 37.7 %all-reduce.19.cloned.1.call-done = f32[2,256,256]{2,1,0:T(8,128)} async-done(((f32[2,256,256]{2,1,0:T(8,128)}), f32[2,256,256]{2,1,0:T(8,128)}) %all-reduce.19.cloned.1.call-update) | async-done | bytes 524304 | tf_op jit(solution)/shard_map/psum | solution.py:155
  263.8 7.8 dynamic_update_slice.26
  273.6 8.2 %dynamic_update_slice.27 = f32[2,384,512]{1,2,0:T(8,128)S(1)} dynamic-update-slice(f32[2,384,512]{1,2,0:T(8,128)S(1)} %dynamic_update_slice.26, f32[2,256,256]{1,2,0:T(8,128)} %fusion.47, s32[]{:T(128)} %constant.15.clone.1, s32[]{:T(128)S(6)} %select_n.33, s32[]{:T(128)S(6)} %select_n.34) | dynamic-update-slice | bytes 1048580 | tf_op jit(solution)/shard_map/dynamic_update_slice | solution.py:166
  291.8 12.9 %collective-permute-done.14 = f32[2,640,128]{1,2,0:T(8,128)S(1)} collective-permute-done((f32[2,640,128]{1,2,0:T(8,128)S(1)}, f32[2,640,128]{1,2,0:T(8,128)S(1)}, u32[]{:S(2)}, u32[]{:S(2)}) %collective-permute-start.14) | collective-permute-done | bytes 655392 | tf_op jit(solution)/shard_map/ppermute | solution.py:16
  304.7 16.7 %collective-permute-done.15 = f32[2,640,128]{1,2,0:T(8,128)S(1)} collective-permute-done((f32[2,640,128]{1,2,0:T(8,128)S(1)}, f32[2,640,128]{1,2,0:T(8,128)S(1)}, u32[]{:S(2)}, u32[]{:S(2)}) %collective-permute-start.15) | collective-permute-done | bytes 655392 | tf_op jit(solution)/shard_map/ppermute | solution.py:19
  322.6 33.6 %all-reduce.21.cloned.1.call-done = f32[2,128,256]{1,2,0:T(8,128)} async-done(((f32[2,128,256]{1,2,0:T(8,128)}), f32[2,128,256]{1,2,0:T(8,128)}) %all-reduce.21.cloned.1.call-update) | async-done | bytes 262160 | tf_op jit(solution)/shard_map/psum | solution.py:158
  357.9 40.4 %all-reduce.5 = (f32[]{:T(128)}, f32[]{:T(128)}) all-reduce(f32[]{:T(128)} %get-tuple-element.16, f32[]{:T(128)} %get-tuple-element.15), channel_id=1, replica_groups=mesh['gx'=2,'gy'=4,'ma'=4] {'gx','gy','ma'}, use_global_device_ids=true, to_apply=%region_6.7 | all-reduce | flops 2 | bytes 16 | tf_op jit(solution)/shard_map/psum | solution.py:193
  410.1 7.3 collective-permute-done.18
  417.4 10.6 %collective-permute-done.19 = f32[2,384,128]{1,2,0:T(8,128)S(1)} collective-permute-done((f32[2,384,128]{1,2,0:T(8,128)S(1)}, f32[2,384,128]{1,2,0:T(8,128)S(1)}, u32[]{:S(2)}, u32[]{:S(2)}) %collective-permute-start.19) | collective-permute-done | bytes 393248 | tf_op jit(solution)/shard_map/ppermute | solution.py:19
  435.4 36.2 %all-reduce.23.cloned.1.call-done = f32[2,256,256]{2,1,0:T(8,128)} async-done(((f32[2,256,256]{2,1,0:T(8,128)}), f32[2,256,256]{2,1,0:T(8,128)}) %all-reduce.23.cloned.1.call-update) | async-done | bytes 524304 | tf_op jit(solution)/shard_map/psum | solution.py:155
  479.5 7.8 dynamic_update_slice.28
  489.3 8.2 %dynamic_update_slice.29 = f32[2,384,512]{1,2,0:T(8,128)S(1)} dynamic-update-slice(f32[2,384,512]{1,2,0:T(8,128)S(1)} %dynamic_update_slice.28, f32[2,256,256]{1,2,0:T(8,128)} %fusion.44, s32[]{:T(128)} %constant.15.clone.1, s32[]{:T(128)S(6)} %select_n.33, s32[]{:T(128)S(6)} %select_n.34) | dynamic-update-slice | bytes 1048580 | tf_op jit(solution)/shard_map/dynamic_update_slice | solution.py:166
  507.4 12.9 %collective-permute-done.22 = f32[2,640,128]{1,2,0:T(8,128)S(1)} collective-permute-done((f32[2,640,128]{1,2,0:T(8,128)S(1)}, f32[2,640,128]{1,2,0:T(8,128)S(1)}, u32[]{:S(2)}, u32[]{:S(2)}) %collective-permute-start.22) | collective-permute-done | bytes 655392 | tf_op jit(solution)/shard_map/ppermute | solution.py:16
  520.4 16.7 %collective-permute-done.23 = f32[2,640,128]{1,2,0:T(8,128)S(1)} collective-permute-done((f32[2,640,128]{1,2,0:T(8,128)S(1)}, f32[2,640,128]{1,2,0:T(8,128)S(1)}, u32[]{:S(2)}, u32[]{:S(2)}) %collective-permute-start.23) | collective-permute-done | bytes 655392 | tf_op jit(solution)/shard_map/ppermute | solution.py:19
  538.0 33.7 %all-reduce.25.cloned.1.call-done = f32[2,128,256]{1,2,0:T(8,128)} async-done(((f32[2,128,256]{1,2,0:T(8,128)}), f32[2,128,256]{1,2,0:T(8,128)}) %all-reduce.25.cloned.1.call-update) | async-done | bytes 262160 | tf_op jit(solution)/shard_map/psum | solution.py:158
  582.3 7.3 collective-permute-done.26
  589.6 10.3 %collective-permute-done.27 = f32[2,384,128]{1,2,0:T(8,128)S(1)} collective-permute-done((f32[2,384,128]{1,2,0:T(8,128)S(1)}, f32[2,384,128]{1,2,0:T(8,128)S(1)}, u32[]{:S(2)}, u32[]{:S(2)}) %collective-permute-start.27) | collective-permute-done | bytes 393248 | tf_op jit(solution)/shard_map/ppermute | solution.py:19
  607.7 37.7 %all-reduce.27.cloned.1.call-done = f32[2,256,256]{2,1,0:T(8,128)} async-done(((f32[2,256,256]{2,1,0:T(8,128)}), f32[2,256,256]{2,1,0:T(8,128)}) %all-reduce.27.cloned.1.call-update) | async-done | bytes 524304 | tf_op jit(solution)/shard_map/psum | solution.py:155
  653.0 8.2 %dynamic_update_slice.30 = f32[2,384,512]{1,2,0:T(8,128)S(1)} dynamic-update-slice(f32[2,384,512]{1,2,0:T(8,128)S(1)} %broadcast.214, f32[2,256,256]{1,2,0:T(8,128)S(1)} %fusion.25, s32[]{:T(128)} %constant.15.clone.1, s32[]{:T(128)S(6)} %select_n.31, s32[]{:T(128)S(6)} %select_n.32) | dynamic-update-slice | bytes 1048580 | tf_op jit(solution)/shard_map/dynamic_update_slice | solution.py:166
  662.4 8.8 %dynamic_update_slice.31 = f32[2,384,512]{1,2,0:T(8,128)S(1)} dynamic-update-slice(f32[2,384,512]{1,2,0:T(8,128)S(1)} %dynamic_update_slice.30, f32[2,256,256]{1,2,0:T(8,128)S(1)} %fusion.41, s32[]{:T(128)} %constant.15.clone.1, s32[]{:T(128)S(6)} %select_n.33, s32[]{:T(128)S(6)} %select_n.34) | dynamic-update-slice | bytes 1048580 | tf_op jit(solution)/shard_map/dynamic_update_slice | solution.py:166
  681.1 12.9 %collective-permute-done.30 = f32[2,640,128]{1,2,0:T(8,128)S(1)} collective-permute-done((f32[2,640,128]{1,2,0:T(8,128)S(1)}, f32[2,640,128]{1,2,0:T(8,128)S(1)}, u32[]{:S(2)}, u32[]{:S(2)}) %collective-permute-start.30) | collective-permute-done | bytes 655392 | tf_op jit(solution)/shard_map/ppermute | solution.py:16
  694.1 16.9 %collective-permute-done.31 = f32[2,640,128]{1,2,0:T(8,128)S(1)} collective-permute-done((f32[2,640,128]{1,2,0:T(8,128)S(1)}, f32[2,640,128]{1,2,0:T(8,128)S(1)}, u32[]{:S(2)}, u32[]{:S(2)}) %collective-permute-start.31) | collective-permute-done | bytes 655392 | tf_op jit(solution)/shard_map/ppermute | solution.py:19
  712.0 33.7 %all-reduce.29.cloned.1.call-done = f32[2,128,256]{1,2,0:T(8,128)} async-done(((f32[2,128,256]{1,2,0:T(8,128)}), f32[2,128,256]{1,2,0:T(8,128)}) %all-reduce.29.cloned.1.call-update) | async-done | bytes 262160 | tf_op jit(solution)/shard_map/psum | solution.py:158
  747.6 40.4 %all-reduce.4 = (f32[]{:T(128)}, f32[]{:T(128)}) all-reduce(f32[]{:T(128)} %get-tuple-element.14, f32[]{:T(128)} %get-tuple-element.13), channel_id=1, replica_groups=mesh['gx'=2,'gy'=4,'ma'=4] {'gx','gy','ma'}, use_global_device_ids=true, to_apply=%region_20.21 | all-reduce | flops 2 | bytes 16 | tf_op jit(solution)/shard_map/psum | solution.py:193
  (264 shorter events, 170.7 us)
Async XLA Ops:
  6.5 75.1 %all-reduce.15.cloned.1.call-start = ((), (), s32[]{:S(2)}) async-start(), calls=%async_computation | async-start | bytes 1048576 | tf_op jit(solution)/shard_map/psum | solution.py:155
  6.5 5.2 collective-permute-start
  9.1 3.6 collective-permute-start.1
  13.7 17.3 %collective-permute-start.2 = (f32[2,384,128]{2,1,0:T(8,128)}, f32[2,384,128]{2,1,0:T(8,128)S(1)}, u32[]{:S(2)}, u32[]{:S(2)}) collective-permute-start(f32[2,384,128]{2,1,0:T(8,128)} %get-tuple-element.69), channel_id=1, source_target_pairs={{0,4},{4,8},{8,12},{1,5},{5,9},{9,13},{2,6},{6,10},{10,14},{3,7},{... | collective-permute-start | bytes 1179656 | tf_op jit(solution)/shard_map/ppermute | solution.py:16
  17.9 19.4 %collective-permute-start.3 = (f32[2,384,128]{2,1,0:T(8,128)}, f32[2,384,128]{2,1,0:T(8,128)}, u32[]{:S(2)}, u32[]{:S(2)}) collective-permute-start(f32[2,384,128]{2,1,0:T(8,128)} %get-tuple-element.70), channel_id=1, source_target_pairs={{4,0},{8,4},{12,8},{5,1},{9,5},{13,9},{6,2},{10,6},{14,10},{7,3},{... | collective-permute-start | bytes 1179656 | tf_op jit(solution)/shard_map/ppermute | solution.py:19
  42.5 139.8 %all-reduce.17.cloned.1.call-start = ((), (), s32[]{:S(2)}) async-start(), calls=%async_computation.1 | async-start | bytes 524288 | tf_op jit(solution)/shard_map/psum | solution.py:158
  108.9 3.8 collective-permute-start.5
  112.8 17.5 %collective-permute-start.6 = (f32[2,640,128]{1,2,0:T(8,128)S(1)}, f32[2,640,128]{1,2,0:T(8,128)S(1)}, u32[]{:S(2)}, u32[]{:S(2)}) collective-permute-start(f32[2,640,128]{1,2,0:T(8,128)S(1)} %get-tuple-element.27), channel_id=1, source_target_pairs={{0,4},{4,8},{8,12},{1,5},{5,9},{9,13},{2,6},{6,10},{10,14},{3,7},{... | collective-permute-start | bytes 1966088 | tf_op jit(solution)/shard_map/ppermute | solution.py:16
  116.1 30.9 %collective-permute-start.7 = (f32[2,640,128]{1,2,0:T(8,128)S(1)}, f32[2,640,128]{1,2,0:T(8,128)S(1)}, u32[]{:S(2)}, u32[]{:S(2)}) collective-permute-start(f32[2,640,128]{1,2,0:T(8,128)S(1)} %get-tuple-element.28), channel_id=1, source_target_pairs={{4,0},{8,4},{12,8},{5,1},{9,5},{13,9},{6,2},{10,6},{14,10},{7,3},{... | collective-permute-start | bytes 1966088 | tf_op jit(solution)/shard_map/ppermute | solution.py:19
  148.5 107.5 %all-reduce.19.cloned.1.call-start = ((), (), s32[]{:S(2)}) async-start(), calls=%async_computation.2 | async-start | bytes 1048576 | tf_op jit(solution)/shard_map/psum | solution.py:155
  184.6 3.4 collective-permute-start.9
  188.2 12.0 %collective-permute-start.10 = (f32[2,384,128]{1,2,0:T(8,128)S(1)}, f32[2,384,128]{1,2,0:T(8,128)S(1)}, u32[]{:S(2)}, u32[]{:S(2)}) collective-permute-start(f32[2,384,128]{1,2,0:T(8,128)S(1)} %get-tuple-element.67), channel_id=1, source_target_pairs={{0,4},{4,8},{8,12},{1,5},{5,9},{9,13},{2,6},{6,10},{10,14},{3,7},{... | collective-permute-start | bytes 1179656 | tf_op jit(solution)/shard_map/ppermute | solution.py:16
  191.6 19.0 %collective-permute-start.11 = (f32[2,384,128]{1,2,0:T(8,128)S(1)}, f32[2,384,128]{1,2,0:T(8,128)S(1)}, u32[]{:S(2)}, u32[]{:S(2)}) collective-permute-start(f32[2,384,128]{1,2,0:T(8,128)S(1)} %get-tuple-element.68), channel_id=1, source_target_pairs={{4,0},{8,4},{12,8},{5,1},{9,5},{13,9},{6,2},{10,6},{14,10},{7,3},{... | collective-permute-start | bytes 1179656 | tf_op jit(solution)/shard_map/ppermute | solution.py:19
  218.2 137.9 %all-reduce.21.cloned.1.call-start = ((), (), s32[]{:S(2)}) async-start(), calls=%async_computation.3 | async-start | bytes 524288 | tf_op jit(solution)/shard_map/psum | solution.py:158
  283.3 3.8 collective-permute-start.13
  287.2 17.5 %collective-permute-start.14 = (f32[2,640,128]{1,2,0:T(8,128)S(1)}, f32[2,640,128]{1,2,0:T(8,128)S(1)}, u32[]{:S(2)}, u32[]{:S(2)}) collective-permute-start(f32[2,640,128]{1,2,0:T(8,128)S(1)} %get-tuple-element.25), channel_id=1, source_target_pairs={{0,4},{4,8},{8,12},{1,5},{5,9},{9,13},{2,6},{6,10},{10,14},{3,7},{... | collective-permute-start | bytes 1966088 | tf_op jit(solution)/shard_map/ppermute | solution.py:16
  290.5 30.9 %collective-permute-start.15 = (f32[2,640,128]{1,2,0:T(8,128)S(1)}, f32[2,640,128]{1,2,0:T(8,128)S(1)}, u32[]{:S(2)}, u32[]{:S(2)}) collective-permute-start(f32[2,640,128]{1,2,0:T(8,128)S(1)} %get-tuple-element.26), channel_id=1, source_target_pairs={{4,0},{8,4},{12,8},{5,1},{9,5},{13,9},{6,2},{10,6},{14,10},{7,3},{... | collective-permute-start | bytes 1966088 | tf_op jit(solution)/shard_map/ppermute | solution.py:19
  322.4 149.3 %all-reduce.23.cloned.1.call-start = ((), (), s32[]{:S(2)}) async-start(), calls=%async_computation.4 | async-start | bytes 1048576 | tf_op jit(solution)/shard_map/psum | solution.py:155
  401.0 3.4 collective-permute-start.17
  404.6 12.8 %collective-permute-start.18 = (f32[2,384,128]{1,2,0:T(8,128)S(1)}, f32[2,384,128]{1,2,0:T(8,128)S(1)}, u32[]{:S(2)}, u32[]{:S(2)}) collective-permute-start(f32[2,384,128]{1,2,0:T(8,128)S(1)} %get-tuple-element.65), channel_id=1, source_target_pairs={{0,4},{4,8},{8,12},{1,5},{5,9},{9,13},{2,6},{6,10},{10,14},{3,7},{... | collective-permute-start | bytes 1179656 | tf_op jit(solution)/shard_map/ppermute | solution.py:16
  408.8 19.2 %collective-permute-start.19 = (f32[2,384,128]{1,2,0:T(8,128)S(1)}, f32[2,384,128]{1,2,0:T(8,128)S(1)}, u32[]{:S(2)}, u32[]{:S(2)}) collective-permute-start(f32[2,384,128]{1,2,0:T(8,128)S(1)} %get-tuple-element.66), channel_id=1, source_target_pairs={{4,0},{8,4},{12,8},{5,1},{9,5},{13,9},{6,2},{10,6},{14,10},{7,3},{... | collective-permute-start | bytes 1179656 | tf_op jit(solution)/shard_map/ppermute | solution.py:19
  435.1 136.6 %all-reduce.25.cloned.1.call-start = ((), (), s32[]{:S(2)}) async-start(), calls=%async_computation.5 | async-start | bytes 524288 | tf_op jit(solution)/shard_map/psum | solution.py:158
  498.9 3.8 collective-permute-start.21
  502.8 17.5 %collective-permute-start.22 = (f32[2,640,128]{1,2,0:T(8,128)S(1)}, f32[2,640,128]{1,2,0:T(8,128)S(1)}, u32[]{:S(2)}, u32[]{:S(2)}) collective-permute-start(f32[2,640,128]{1,2,0:T(8,128)S(1)} %get-tuple-element.23), channel_id=1, source_target_pairs={{0,4},{4,8},{8,12},{1,5},{5,9},{9,13},{2,6},{6,10},{10,14},{3,7},{... | collective-permute-start | bytes 1966088 | tf_op jit(solution)/shard_map/ppermute | solution.py:16
  506.1 30.9 %collective-permute-start.23 = (f32[2,640,128]{1,2,0:T(8,128)S(1)}, f32[2,640,128]{1,2,0:T(8,128)S(1)}, u32[]{:S(2)}, u32[]{:S(2)}) collective-permute-start(f32[2,640,128]{1,2,0:T(8,128)S(1)} %get-tuple-element.24), channel_id=1, source_target_pairs={{4,0},{8,4},{12,8},{5,1},{9,5},{13,9},{6,2},{10,6},{14,10},{7,3},{... | collective-permute-start | bytes 1966088 | tf_op jit(solution)/shard_map/ppermute | solution.py:19
  538.0 107.5 %all-reduce.27.cloned.1.call-start = ((), (), s32[]{:S(2)}) async-start(), calls=%async_computation.6 | async-start | bytes 1048576 | tf_op jit(solution)/shard_map/psum | solution.py:155
  577.6 12.0 %collective-permute-start.26 = (f32[2,384,128]{1,2,0:T(8,128)S(1)}, f32[2,384,128]{1,2,0:T(8,128)S(1)}, u32[]{:S(2)}, u32[]{:S(2)}) collective-permute-start(f32[2,384,128]{1,2,0:T(8,128)S(1)} %get-tuple-element.63), channel_id=1, source_target_pairs={{0,4},{4,8},{8,12},{1,5},{5,9},{9,13},{2,6},{6,10},{10,14},{3,7},{... | collective-permute-start | bytes 1179656 | tf_op jit(solution)/shard_map/ppermute | solution.py:16
  581.0 19.0 %collective-permute-start.27 = (f32[2,384,128]{1,2,0:T(8,128)S(1)}, f32[2,384,128]{1,2,0:T(8,128)S(1)}, u32[]{:S(2)}, u32[]{:S(2)}) collective-permute-start(f32[2,384,128]{1,2,0:T(8,128)S(1)} %get-tuple-element.64), channel_id=1, source_target_pairs={{4,0},{8,4},{12,8},{5,1},{9,5},{13,9},{6,2},{10,6},{14,10},{7,3},{... | collective-permute-start | bytes 1179656 | tf_op jit(solution)/shard_map/ppermute | solution.py:19
  607.7 138.1 %all-reduce.29.cloned.1.call-start = ((), (), s32[]{:S(2)}) async-start(), calls=%async_computation.7 | async-start | bytes 524288 | tf_op jit(solution)/shard_map/psum | solution.py:158
  672.7 3.8 collective-permute-start.29
  676.6 17.5 %collective-permute-start.30 = (f32[2,640,128]{1,2,0:T(8,128)S(1)}, f32[2,640,128]{1,2,0:T(8,128)S(1)}, u32[]{:S(2)}, u32[]{:S(2)}) collective-permute-start(f32[2,640,128]{1,2,0:T(8,128)S(1)} %get-tuple-element.21), channel_id=1, source_target_pairs={{0,4},{4,8},{8,12},{1,5},{5,9},{9,13},{2,6},{6,10},{10,14},{3,7},{... | collective-permute-start | bytes 1966088 | tf_op jit(solution)/shard_map/ppermute | solution.py:16
  679.8 31.2 %collective-permute-start.31 = (f32[2,640,128]{1,2,0:T(8,128)S(1)}, f32[2,640,128]{1,2,0:T(8,128)S(1)}, u32[]{:S(2)}, u32[]{:S(2)}) collective-permute-start(f32[2,640,128]{1,2,0:T(8,128)S(1)} %get-tuple-element.22), channel_id=1, source_target_pairs={{4,0},{8,4},{12,8},{5,1},{9,5},{13,9},{6,2},{10,6},{14,10},{7,3},{... | collective-permute-start | bytes 1966088 | tf_op jit(solution)/shard_map/ppermute | solution.py:19
  (41 other events, 427.5 us)
Sparse Core Ops, SparseCore 0:
  42.6 38.9 all-reduce.14
  148.7 33.5 all-reduce.16
  218.4 37.6 all-reduce.18
  322.5 33.5 all-reduce.20
  435.2 36.3 all-reduce.22
  538.1 33.5 all-reduce.24
  607.8 37.6 all-reduce.26
  712.1 33.5 all-reduce.28
where the time goes:
time: 808 us; the launch traced here: 797 us
  waiting for transfers between devices  478 us (59%)
  local copies, waits for them, and re-layouts  94.4 us (12%)
  blocking collectives  80.8 us (10%)
  starting transfers between devices  61.5 us (8%)
  other arithmetic  40.6 us (5%)
  between operations  26.1 us (3%)
  matrix products  15.7 us (2%)
    psum x4, waiting for transfers between devices, mode_total(): return lax.psum(partial_value, 'ma')  148 us
    psum x4, waiting for transfers between devices, combine(): summed = lax.psum(folded, 'ma')  135 us
    ppermute x16, waiting for transfers between devices, padded_2(): lax.ppermute(lax.slice_in_dim(block, 0, width, axis=dim), axis, backward)  121 us
    psum x2, blocking collectives, shards(): norm_now = lax.psum(local_sum(residual, residual), ('gx', 'gy', 'ma'))  80.8 us
    ppermute x16, waiting for transfers between devices, padded_2(): lax.ppermute(lax.slice_in_dim(block, block.shape[dim] - width, None, axis...  74.3 us
    dynamic_update_slice x8, local copies, waits for them, and re-layouts, project(): lax.dynamic_update_slice(extended, lax.dynamic_slice(extended, corner, (2...  65.2 us
    ppermute x16, starting transfers between devices, padded_2(): lax.ppermute(lax.slice_in_dim(block, block.shape[dim] - width, None, axis...  40.1 us
    ppermute x16, starting transfers between devices, padded_2(): lax.ppermute(lax.slice_in_dim(block, 0, width, axis=dim), axis, backward)  20.8 us
  transfers between devices with their start and end apart: 40, of which 35 were waited for; matrix products, arithmetic and copies ran while one was open for 1% of the time, Pallas kernels for 0%

commit v1 on v0

--- a/solution.py
+++ b/solution.py
@@ -3,6 +3,7 @@
 import jax.numpy as jnp
 from jax import lax
 from jax.sharding import PartitionSpec as P
+from jax.lax import psum
 
 OUTER = 2
 DAMPING = 1.0
@@ -190,7 +191,9 @@
         gradient = project(misfit, spectra)
         residual = -gradient
         direction = residual
-        norm_now = lax.psum(local_sum(residual, residual), ("gx", "gy", "ma"))
+        vals = local_sum(residual, residual)
+        main = psum(vals, ("gy", "ma"))
+        norm_now = psum(main, axis_name="gx")
         moved_spectra = spectra_of(direction)
         change = live_mask * mode_total(change_part(spectra, moved_spectra, mode_count))
         applied = project(change, spectra) + DAMPING * direction

time: 808 us -> 892 us (1.10)
  blocking collectives: 80.8 us -> 163 us
    psum x2 -> x6, blocking collectives: 80.8 us -> 163 us  [the longest x2 82.9 us: shards(): main = psum(vals, ('gy', 'ma'))]
where the time goes in v1:
time: 892 us; the launch traced here: 881 us
  waiting for transfers between devices  479 us (54%)
  blocking collectives  163 us (18%)
  local copies, waits for them, and re-layouts  94.5 us (11%)
  starting transfers between devices  61.4 us (7%)
  other arithmetic  40.5 us (5%)
  between operations  26 us (3%)
  matrix products  15.7 us (2%)
    psum x4, waiting for transfers between devices, mode_total(): return lax.psum(partial_value, 'ma')  149 us
    psum x4, waiting for transfers between devices, combine(): summed = lax.psum(folded, 'ma')  135 us
    ppermute x16, waiting for transfers between devices, padded_2(): lax.ppermute(lax.slice_in_dim(block, 0, width, axis=dim), axis, backward)  121 us
    psum x2, blocking collectives, shards(): main = psum(vals, ('gy', 'ma'))  82.9 us
    ppermute x16, waiting for transfers between devices, padded_2(): lax.ppermute(lax.slice_in_dim(block, block.shape[dim] - width, None, axis...  74.3 us
    psum x2, blocking collectives, shards(): lax.psum(local_sum(direction, applied), ('gx', 'gy', 'ma'))  74 us
    dynamic_update_slice x8, local copies, waits for them, and re-layouts, project(): lax.dynamic_update_slice(extended, lax.dynamic_slice(extended, corner, (2...  65.2 us
    ppermute x16, starting transfers between devices, padded_2(): lax.ppermute(lax.slice_in_dim(block, block.shape[dim] - width, None, axis...  40.1 us
  transfers between devices with their start and end apart: 40, of which 35 were waited for; matrix products, arithmetic and copies ran while one was open for 1% of the time, Pallas kernels for 0%

profile of v1, /device:TPU:0, one launch (start us, length us, event | category | flops | bytes accessed | tf_op | source)
XLA Modules:
  0.0 880.6 jit_solution(12997406391595646566)
XLA Ops:
  45.2 36.4 %all-reduce.13.cloned.1.call-done = f32[2,256,256]{2,1,0:T(8,128)} async-done(((f32[2,256,256]{2,1,0:T(8,128)}), f32[2,256,256]{2,1,0:T(8,128)}) %all-reduce.13.cloned.1.call-update) | async-done | bytes 524304 | tf_op jit(solution)/shard_map/psum | solution.py:156
  89.6 7.8 dynamic_update_slice.24
  99.4 8.2 dynamic_update_slice.25
  117.5 12.9 %collective-permute-done.6 = f32[2,640,128]{1,2,0:T(8,128)S(1)} collective-permute-done((f32[2,640,128]{1,2,0:T(8,128)S(1)}, f32[2,640,128]{1,2,0:T(8,128)S(1)}, u32[]{:S(2)}, u32[]{:S(2)}) %collective-permute-start.6) | collective-permute-done | bytes 655392 | tf_op jit(solution)/shard_map/ppermute | solution.py:17
  130.5 16.7 %collective-permute-done.7 = f32[2,640,128]{1,2,0:T(8,128)S(1)} collective-permute-done((f32[2,640,128]{1,2,0:T(8,128)S(1)}, f32[2,640,128]{1,2,0:T(8,128)S(1)}, u32[]{:S(2)}, u32[]{:S(2)}) %collective-permute-start.7) | collective-permute-done | bytes 655392 | tf_op jit(solution)/shard_map/ppermute | solution.py:20
  148.7 33.7 %all-reduce.15.cloned.1.call-done = f32[2,128,256]{1,2,0:T(8,128)} async-done(((f32[2,128,256]{1,2,0:T(8,128)}), f32[2,128,256]{1,2,0:T(8,128)}) %all-reduce.15.cloned.1.call-update) | async-done | bytes 262160 | tf_op jit(solution)/shard_map/psum | solution.py:159
  200.3 10.3 %collective-permute-done.11 = f32[2,384,128]{1,2,0:T(8,128)S(1)} collective-permute-done((f32[2,384,128]{1,2,0:T(8,128)S(1)}, f32[2,384,128]{1,2,0:T(8,128)S(1)}, u32[]{:S(2)}, u32[]{:S(2)}) %collective-permute-start.11) | collective-permute-done | bytes 393248 | tf_op jit(solution)/shard_map/ppermute | solution.py:20
  218.4 37.7 %all-reduce.17.cloned.1.call-done = f32[2,256,256]{2,1,0:T(8,128)} async-done(((f32[2,256,256]{2,1,0:T(8,128)}), f32[2,256,256]{2,1,0:T(8,128)}) %all-reduce.17.cloned.1.call-update) | async-done | bytes 524304 | tf_op jit(solution)/shard_map/psum | solution.py:156
  263.8 7.8 dynamic_update_slice.26
  273.6 8.2 dynamic_update_slice.27
  291.8 12.9 %collective-permute-done.14 = f32[2,640,128]{1,2,0:T(8,128)S(1)} collective-permute-done((f32[2,640,128]{1,2,0:T(8,128)S(1)}, f32[2,640,128]{1,2,0:T(8,128)S(1)}, u32[]{:S(2)}, u32[]{:S(2)}) %collective-permute-start.14) | collective-permute-done | bytes 655392 | tf_op jit(solution)/shard_map/ppermute | solution.py:17
  304.7 16.7 %collective-permute-done.15 = f32[2,640,128]{1,2,0:T(8,128)S(1)} collective-permute-done((f32[2,640,128]{1,2,0:T(8,128)S(1)}, f32[2,640,128]{1,2,0:T(8,128)S(1)}, u32[]{:S(2)}, u32[]{:S(2)}) %collective-permute-start.15) | collective-permute-done | bytes 655392 | tf_op jit(solution)/shard_map/ppermute | solution.py:20
  322.4 33.7 %all-reduce.19.cloned.1.call-done = f32[2,128,256]{1,2,0:T(8,128)} async-done(((f32[2,128,256]{1,2,0:T(8,128)}), f32[2,128,256]{1,2,0:T(8,128)}) %all-reduce.19.cloned.1.call-update) | async-done | bytes 262160 | tf_op jit(solution)/shard_map/psum | solution.py:159
  357.9 41.4 %psum.100 = f32[]{:T(128)} all-reduce(f32[]{:T(128)} %get-tuple-element.16), channel_id=1, replica_groups=mesh['gx'=2,'gy'=4,'ma'=4] {'gy','ma'}, use_global_device_ids=true, to_apply=%region_6.7 | all-reduce | flops 1 | bytes 8 | tf_op jit(solution)/shard_map/psum | solution.py:195
  402.4 37.0 %psum.104 = f32[]{:T(128)} all-reduce(f32[]{:T(128)} %get-tuple-element.15), channel_id=1, replica_groups=mesh['gx'=2,'gy'=4,'ma'=4] {'gx','gy','ma'}, use_global_device_ids=true, to_apply=%region_14.15 | all-reduce | flops 1 | bytes 8 | tf_op jit(solution)/shard_map/psum | solution.py:200
  458.5 10.5 %collective-permute-done.19 = f32[2,384,128]{1,2,0:T(8,128)S(1)} collective-permute-done((f32[2,384,128]{1,2,0:T(8,128)S(1)}, f32[2,384,128]{1,2,0:T(8,128)S(1)}, u32[]{:S(2)}, u32[]{:S(2)}) %collective-permute-start.19) | collective-permute-done | bytes 393248 | tf_op jit(solution)/shard_map/ppermute | solution.py:20
  476.4 37.3 %all-reduce.21.cloned.1.call-done = f32[2,256,256]{2,1,0:T(8,128)} async-done(((f32[2,256,256]{2,1,0:T(8,128)}), f32[2,256,256]{2,1,0:T(8,128)}) %all-reduce.21.cloned.1.call-update) | async-done | bytes 524304 | tf_op jit(solution)/shard_map/psum | solution.py:156
  521.6 7.8 dynamic_update_slice.28
  531.4 8.2 dynamic_update_slice.29
  549.5 12.9 %collective-permute-done.22 = f32[2,640,128]{1,2,0:T(8,128)S(1)} collective-permute-done((f32[2,640,128]{1,2,0:T(8,128)S(1)}, f32[2,640,128]{1,2,0:T(8,128)S(1)}, u32[]{:S(2)}, u32[]{:S(2)}) %collective-permute-start.22) | collective-permute-done | bytes 655392 | tf_op jit(solution)/shard_map/ppermute | solution.py:17
  562.5 16.7 %collective-permute-done.23 = f32[2,640,128]{1,2,0:T(8,128)S(1)} collective-permute-done((f32[2,640,128]{1,2,0:T(8,128)S(1)}, f32[2,640,128]{1,2,0:T(8,128)S(1)}, u32[]{:S(2)}, u32[]{:S(2)}) %collective-permute-start.23) | collective-permute-done | bytes 655392 | tf_op jit(solution)/shard_map/ppermute | solution.py:20
  580.2 33.7 %all-reduce.23.cloned.1.call-done = f32[2,128,256]{1,2,0:T(8,128)} async-done(((f32[2,128,256]{1,2,0:T(8,128)}), f32[2,128,256]{1,2,0:T(8,128)}) %all-reduce.23.cloned.1.call-update) | async-done | bytes 262160 | tf_op jit(solution)/shard_map/psum | solution.py:159
  624.4 7.3 collective-permute-done.26
  631.8 10.3 %collective-permute-done.27 = f32[2,384,128]{1,2,0:T(8,128)S(1)} collective-permute-done((f32[2,384,128]{1,2,0:T(8,128)S(1)}, f32[2,384,128]{1,2,0:T(8,128)S(1)}, u32[]{:S(2)}, u32[]{:S(2)}) %collective-permute-start.27) | collective-permute-done | bytes 393248 | tf_op jit(solution)/shard_map/ppermute | solution.py:20
  649.8 37.7 %all-reduce.25.cloned.1.call-done = f32[2,256,256]{2,1,0:T(8,128)} async-done(((f32[2,256,256]{2,1,0:T(8,128)}), f32[2,256,256]{2,1,0:T(8,128)}) %all-reduce.25.cloned.1.call-update) | async-done | bytes 524304 | tf_op jit(solution)/shard_map/psum | solution.py:156
  695.1 8.2 dynamic_update_slice.30
  704.5 8.8 %dynamic_update_slice.31 = f32[2,384,512]{1,2,0:T(8,128)S(1)} dynamic-update-slice(f32[2,384,512]{1,2,0:T(8,128)S(1)} %dynamic_update_slice.30, f32[2,256,256]{1,2,0:T(8,128)S(1)} %fusion.41, s32[]{:T(128)} %constant.15.clone.1, s32[]{:T(128)S(6)} %select_n.33, s32[]{:T(128)S(6)} %select_n.34) | dynamic-update-slice | bytes 1048580 | tf_op jit(solution)/shard_map/dynamic_update_slice | solution.py:167
  723.2 12.9 %collective-permute-done.30 = f32[2,640,128]{1,2,0:T(8,128)S(1)} collective-permute-done((f32[2,640,128]{1,2,0:T(8,128)S(1)}, f32[2,640,128]{1,2,0:T(8,128)S(1)}, u32[]{:S(2)}, u32[]{:S(2)}) %collective-permute-start.30) | collective-permute-done | bytes 655392 | tf_op jit(solution)/shard_map/ppermute | solution.py:17
  736.1 16.9 %collective-permute-done.31 = f32[2,640,128]{1,2,0:T(8,128)S(1)} collective-permute-done((f32[2,640,128]{1,2,0:T(8,128)S(1)}, f32[2,640,128]{1,2,0:T(8,128)S(1)}, u32[]{:S(2)}, u32[]{:S(2)}) %collective-permute-start.31) | collective-permute-done | bytes 655392 | tf_op jit(solution)/shard_map/ppermute | solution.py:20
  754.0 33.8 %all-reduce.27.cloned.1.call-done = f32[2,128,256]{1,2,0:T(8,128)} async-done(((f32[2,128,256]{1,2,0:T(8,128)}), f32[2,128,256]{1,2,0:T(8,128)}) %all-reduce.27.cloned.1.call-update) | async-done | bytes 262160 | tf_op jit(solution)/shard_map/psum | solution.py:159
  789.6 41.5 %psum.107 = f32[]{:T(128)} all-reduce(f32[]{:T(128)} %get-tuple-element.14), channel_id=1, replica_groups=mesh['gx'=2,'gy'=4,'ma'=4] {'gy','ma'}, use_global_device_ids=true, to_apply=%region_21.22 | all-reduce | flops 1 | bytes 8 | tf_op jit(solution)/shard_map/psum | solution.py:195
  834.3 37.0 %psum.111 = f32[]{:T(128)} all-reduce(f32[]{:T(128)} %get-tuple-element.13), channel_id=1, replica_groups=mesh['gx'=2,'gy'=4,'ma'=4] {'gx','gy','ma'}, use_global_device_ids=true, to_apply=%region_29.30 | all-reduce | flops 1 | bytes 8 | tf_op jit(solution)/shard_map/psum | solution.py:200
  (268 shorter events, 191.2 us)
Async XLA Ops:
  6.5 75.1 %all-reduce.13.cloned.1.call-start = ((), (), s32[]{:S(2)}) async-start(), calls=%async_computation | async-start | bytes 1048576 | tf_op jit(solution)/shard_map/psum | solution.py:156
  6.5 5.2 collective-permute-start
  9.1 3.6 collective-permute-start.1
  13.7 17.4 %collective-permute-start.2 = (f32[2,384,128]{2,1,0:T(8,128)}, f32[2,384,128]{2,1,0:T(8,128)S(1)}, u32[]{:S(2)}, u32[]{:S(2)}) collective-permute-start(f32[2,384,128]{2,1,0:T(8,128)} %get-tuple-element.65), channel_id=1, source_target_pairs={{0,4},{4,8},{8,12},{1,5},{5,9},{9,13},{2,6},{6,10},{10,14},{3,7},{... | collective-permute-start | bytes 1179656 | tf_op jit(solution)/shard_map/ppermute | solution.py:17
  17.9 19.4 %collective-permute-start.3 = (f32[2,384,128]{2,1,0:T(8,128)}, f32[2,384,128]{2,1,0:T(8,128)}, u32[]{:S(2)}, u32[]{:S(2)}) collective-permute-start(f32[2,384,128]{2,1,0:T(8,128)} %get-tuple-element.66), channel_id=1, source_target_pairs={{4,0},{8,4},{12,8},{5,1},{9,5},{13,9},{6,2},{10,6},{14,10},{7,3},{... | collective-permute-start | bytes 1179656 | tf_op jit(solution)/shard_map/ppermute | solution.py:20
  42.5 139.9 %all-reduce.15.cloned.1.call-start = ((), (), s32[]{:S(2)}) async-start(), calls=%async_computation.1 | async-start | bytes 524288 | tf_op jit(solution)/shard_map/psum | solution.py:159
  109.0 3.8 collective-permute-start.5
  112.9 17.5 %collective-permute-start.6 = (f32[2,640,128]{1,2,0:T(8,128)S(1)}, f32[2,640,128]{1,2,0:T(8,128)S(1)}, u32[]{:S(2)}, u32[]{:S(2)}) collective-permute-start(f32[2,640,128]{1,2,0:T(8,128)S(1)} %get-tuple-element.23), channel_id=1, source_target_pairs={{0,4},{4,8},{8,12},{1,5},{5,9},{9,13},{2,6},{6,10},{10,14},{3,7},{... | collective-permute-start | bytes 1966088 | tf_op jit(solution)/shard_map/ppermute | solution.py:17
  116.2 30.9 %collective-permute-start.7 = (f32[2,640,128]{1,2,0:T(8,128)S(1)}, f32[2,640,128]{1,2,0:T(8,128)S(1)}, u32[]{:S(2)}, u32[]{:S(2)}) collective-permute-start(f32[2,640,128]{1,2,0:T(8,128)S(1)} %get-tuple-element.24), channel_id=1, source_target_pairs={{4,0},{8,4},{12,8},{5,1},{9,5},{13,9},{6,2},{10,6},{14,10},{7,3},{... | collective-permute-start | bytes 1966088 | tf_op jit(solution)/shard_map/ppermute | solution.py:20
  148.6 107.5 %all-reduce.17.cloned.1.call-start = ((), (), s32[]{:S(2)}) async-start(), calls=%async_computation.2 | async-start | bytes 1048576 | tf_op jit(solution)/shard_map/psum | solution.py:156
  188.2 12.0 %collective-permute-start.10 = (f32[2,384,128]{1,2,0:T(8,128)S(1)}, f32[2,384,128]{1,2,0:T(8,128)S(1)}, u32[]{:S(2)}, u32[]{:S(2)}) collective-permute-start(f32[2,384,128]{1,2,0:T(8,128)S(1)} %get-tuple-element.63), channel_id=1, source_target_pairs={{0,4},{4,8},{8,12},{1,5},{5,9},{9,13},{2,6},{6,10},{10,14},{3,7},{... | collective-permute-start | bytes 1179656 | tf_op jit(solution)/shard_map/ppermute | solution.py:17
  191.6 19.0 %collective-permute-start.11 = (f32[2,384,128]{1,2,0:T(8,128)S(1)}, f32[2,384,128]{1,2,0:T(8,128)S(1)}, u32[]{:S(2)}, u32[]{:S(2)}) collective-permute-start(f32[2,384,128]{1,2,0:T(8,128)S(1)} %get-tuple-element.64), channel_id=1, source_target_pairs={{4,0},{8,4},{12,8},{5,1},{9,5},{13,9},{6,2},{10,6},{14,10},{7,3},{... | collective-permute-start | bytes 1179656 | tf_op jit(solution)/shard_map/ppermute | solution.py:20
  218.3 137.8 %all-reduce.19.cloned.1.call-start = ((), (), s32[]{:S(2)}) async-start(), calls=%async_computation.3 | async-start | bytes 524288 | tf_op jit(solution)/shard_map/psum | solution.py:159
  283.3 3.8 collective-permute-start.13
  287.2 17.5 %collective-permute-start.14 = (f32[2,640,128]{1,2,0:T(8,128)S(1)}, f32[2,640,128]{1,2,0:T(8,128)S(1)}, u32[]{:S(2)}, u32[]{:S(2)}) collective-permute-start(f32[2,640,128]{1,2,0:T(8,128)S(1)} %get-tuple-element.21), channel_id=1, source_target_pairs={{0,4},{4,8},{8,12},{1,5},{5,9},{9,13},{2,6},{6,10},{10,14},{3,7},{... | collective-permute-start | bytes 1966088 | tf_op jit(solution)/shard_map/ppermute | solution.py:17
  290.5 30.9 %collective-permute-start.15 = (f32[2,640,128]{1,2,0:T(8,128)S(1)}, f32[2,640,128]{1,2,0:T(8,128)S(1)}, u32[]{:S(2)}, u32[]{:S(2)}) collective-permute-start(f32[2,640,128]{1,2,0:T(8,128)S(1)} %get-tuple-element.22), channel_id=1, source_target_pairs={{4,0},{8,4},{12,8},{5,1},{9,5},{13,9},{6,2},{10,6},{14,10},{7,3},{... | collective-permute-start | bytes 1966088 | tf_op jit(solution)/shard_map/ppermute | solution.py:20
  322.4 191.3 %all-reduce.21.cloned.1.call-start = ((), (), s32[]{:S(2)}) async-start(), calls=%async_computation.4 | async-start | bytes 1048576 | tf_op jit(solution)/shard_map/psum | solution.py:156
  442.1 3.4 collective-permute-start.17
  445.6 12.8 %collective-permute-start.18 = (f32[2,384,128]{1,2,0:T(8,128)S(1)}, f32[2,384,128]{1,2,0:T(8,128)S(1)}, u32[]{:S(2)}, u32[]{:S(2)}) collective-permute-start(f32[2,384,128]{1,2,0:T(8,128)S(1)} %get-tuple-element.61), channel_id=1, source_target_pairs={{0,4},{4,8},{8,12},{1,5},{5,9},{9,13},{2,6},{6,10},{10,14},{3,7},{... | collective-permute-start | bytes 1179656 | tf_op jit(solution)/shard_map/ppermute | solution.py:17
  449.8 19.2 %collective-permute-start.19 = (f32[2,384,128]{1,2,0:T(8,128)S(1)}, f32[2,384,128]{1,2,0:T(8,128)S(1)}, u32[]{:S(2)}, u32[]{:S(2)}) collective-permute-start(f32[2,384,128]{1,2,0:T(8,128)S(1)} %get-tuple-element.62), channel_id=1, source_target_pairs={{4,0},{8,4},{12,8},{5,1},{9,5},{13,9},{6,2},{10,6},{14,10},{7,3},{... | collective-permute-start | bytes 1179656 | tf_op jit(solution)/shard_map/ppermute | solution.py:20
  476.1 137.8 %all-reduce.23.cloned.1.call-start = ((), (), s32[]{:S(2)}) async-start(), calls=%async_computation.5 | async-start | bytes 524288 | tf_op jit(solution)/shard_map/psum | solution.py:159
  541.0 3.8 collective-permute-start.21
  544.9 17.5 %collective-permute-start.22 = (f32[2,640,128]{1,2,0:T(8,128)S(1)}, f32[2,640,128]{1,2,0:T(8,128)S(1)}, u32[]{:S(2)}, u32[]{:S(2)}) collective-permute-start(f32[2,640,128]{1,2,0:T(8,128)S(1)} %get-tuple-element.19), channel_id=1, source_target_pairs={{0,4},{4,8},{8,12},{1,5},{5,9},{9,13},{2,6},{6,10},{10,14},{3,7},{... | collective-permute-start | bytes 1966088 | tf_op jit(solution)/shard_map/ppermute | solution.py:17
  548.2 30.9 %collective-permute-start.23 = (f32[2,640,128]{1,2,0:T(8,128)S(1)}, f32[2,640,128]{1,2,0:T(8,128)S(1)}, u32[]{:S(2)}, u32[]{:S(2)}) collective-permute-start(f32[2,640,128]{1,2,0:T(8,128)S(1)} %get-tuple-element.20), channel_id=1, source_target_pairs={{4,0},{8,4},{12,8},{5,1},{9,5},{13,9},{6,2},{10,6},{14,10},{7,3},{... | collective-permute-start | bytes 1966088 | tf_op jit(solution)/shard_map/ppermute | solution.py:20
  580.1 107.4 %all-reduce.25.cloned.1.call-start = ((), (), s32[]{:S(2)}) async-start(), calls=%async_computation.6 | async-start | bytes 1048576 | tf_op jit(solution)/shard_map/psum | solution.py:156
  616.2 3.4 collective-permute-start.25
  619.7 12.0 %collective-permute-start.26 = (f32[2,384,128]{1,2,0:T(8,128)S(1)}, f32[2,384,128]{1,2,0:T(8,128)S(1)}, u32[]{:S(2)}, u32[]{:S(2)}) collective-permute-start(f32[2,384,128]{1,2,0:T(8,128)S(1)} %get-tuple-element.59), channel_id=1, source_target_pairs={{0,4},{4,8},{8,12},{1,5},{5,9},{9,13},{2,6},{6,10},{10,14},{3,7},{... | collective-permute-start | bytes 1179656 | tf_op jit(solution)/shard_map/ppermute | solution.py:17
  623.1 19.0 %collective-permute-start.27 = (f32[2,384,128]{1,2,0:T(8,128)S(1)}, f32[2,384,128]{1,2,0:T(8,128)S(1)}, u32[]{:S(2)}, u32[]{:S(2)}) collective-permute-start(f32[2,384,128]{1,2,0:T(8,128)S(1)} %get-tuple-element.60), channel_id=1, source_target_pairs={{4,0},{8,4},{12,8},{5,1},{9,5},{13,9},{6,2},{10,6},{14,10},{7,3},{... | collective-permute-start | bytes 1179656 | tf_op jit(solution)/shard_map/ppermute | solution.py:20
  649.8 138.0 %all-reduce.27.cloned.1.call-start = ((), (), s32[]{:S(2)}) async-start(), calls=%async_computation.7 | async-start | bytes 524288 | tf_op jit(solution)/shard_map/psum | solution.py:159
  714.7 3.8 collective-permute-start.29
  718.6 17.5 %collective-permute-start.30 = (f32[2,640,128]{1,2,0:T(8,128)S(1)}, f32[2,640,128]{1,2,0:T(8,128)S(1)}, u32[]{:S(2)}, u32[]{:S(2)}) collective-permute-start(f32[2,640,128]{1,2,0:T(8,128)S(1)} %get-tuple-element.17), channel_id=1, source_target_pairs={{0,4},{4,8},{8,12},{1,5},{5,9},{9,13},{2,6},{6,10},{10,14},{3,7},{... | collective-permute-start | bytes 1966088 | tf_op jit(solution)/shard_map/ppermute | solution.py:17
  721.9 31.1 %collective-permute-start.31 = (f32[2,640,128]{1,2,0:T(8,128)S(1)}, f32[2,640,128]{1,2,0:T(8,128)S(1)}, u32[]{:S(2)}, u32[]{:S(2)}) collective-permute-start(f32[2,640,128]{1,2,0:T(8,128)S(1)} %get-tuple-element.18), channel_id=1, source_target_pairs={{4,0},{8,4},{12,8},{5,1},{9,5},{13,9},{6,2},{10,6},{14,10},{7,3},{... | collective-permute-start | bytes 1966088 | tf_op jit(solution)/shard_map/ppermute | solution.py:20
  (41 other events, 628.6 us)
Sparse Core Ops, SparseCore 0:
  42.6 38.9 all-reduce.12
  148.8 33.5 all-reduce.14
  218.4 37.6 all-reduce.16
  322.5 33.5 all-reduce.18
  476.2 37.3 all-reduce.20
  580.3 33.5 all-reduce.22
  649.9 37.6 all-reduce.24
  754.1 33.5 all-reduce.26
